TPU v7x, 32 devices: a whole 2x2x4 slice. The times are simulated.
32 devices in a mesh: dp: 8 (over z, core), seq: 4 (over y, x).
Axes of the slice: x: 2, y: 2, z: 4, core: 2. Of those that a mesh axis runs over, the one named last changes fastest.
Arguments:
- tokens: bfloat16 [2, 8, 512, 768], P(None, 'dp', 'seq'), may hold values from -6 to 6
- piece_starts: int32 [2, 8, 2], P(None, 'dp'), may hold values from 0 to 256, as said below
- qkv_weight: bfloat16 [768, 2304], P(('dp', 'seq')), may hold values from -0.21875 to 0.21875
- qv_bias: bfloat16 [1536], P(('dp', 'seq')), may hold values from -1.796875 to 1.796875
- out_weight: bfloat16 [768, 768], P(('dp', 'seq')), may hold values from -1.25 to 1.25
- out_bias: bfloat16 [768], P(('dp', 'seq')), may hold values from -1.796875 to 1.796875
- norm1_gain: bfloat16 [768], P(('dp', 'seq')), may hold values from 0.5 to 1.5
- norm1_bias: bfloat16 [768], P(('dp', 'seq')), may hold values from -1.796875 to 1.796875
- up_weight: bfloat16 [768, 3072], P(('dp', 'seq')), may hold values from -0.21875 to 0.21875
- up_bias: bfloat16 [3072], P(('dp', 'seq')), may hold values from -1.796875 to 1.796875
- down_weight: bfloat16 [3072, 768], P(('dp', 'seq')), may hold values from -0.109375 to 0.109375
- down_bias: bfloat16 [768], P(('dp', 'seq')), may hold values from -1.796875 to 1.796875
- norm2_gain: bfloat16 [768], P(('dp', 'seq')), may hold values from 0.5 to 1.5
- norm2_bias: bfloat16 [768], P(('dp', 'seq')), may hold values from -1.796875 to 1.796875
- grad_out: bfloat16 [2, 8, 512, 768], P(None, 'dp', 'seq'), may hold values from -6 to 6
Outputs:
- layer_out: bfloat16 [2, 8, 512, 768], P(None, 'dp', 'seq')
- tokens_grad: float32 [2, 8, 512, 768], P(None, 'dp', 'seq')
- qkv_weight_grad: float32 [768, 2304], P(('dp', 'seq'))
- qv_bias_grad: float32 [1536], P(('dp', 'seq'))
- out_weight_grad: float32 [768, 768], P(('dp', 'seq'))
- out_bias_grad: float32 [768], P(('dp', 'seq'))
- norm1_gain_grad: float32 [768], P(('dp', 'seq'))
- norm1_bias_grad: float32 [768], P(('dp', 'seq'))
- up_weight_grad: float32 [768, 3072], P(('dp', 'seq'))
- up_bias_grad: float32 [3072], P(('dp', 'seq'))
- down_weight_grad: float32 [3072, 768], P(('dp', 'seq'))
- down_bias_grad: float32 [768], P(('dp', 'seq'))
- norm2_gain_grad: float32 [768], P(('dp', 'seq'))
- norm2_bias_grad: float32 [768], P(('dp', 'seq'))
Inputs may be any that keep to these rules, and one draw needn't show every extreme that they name: `piece_starts`: each sequence's 2 pieces of 256 positions lie inside it, in rising order, without intersection.
All inputs are finite; a program needn't handle non-finite values.
Results may differ from a plain program's by a relative error of at most 0.018.
Values may be sent and summed in bfloat16 or wider, within the bound.
A program may use at most 192 MiB of HBM per device.

v0:
```python
import math
import jax
import jax.numpy as jnp
from jax import lax
from jax.sharding import PartitionSpec as P

HEADS = 12
PIC = 256
NEG = -1e30
EPS = 1e-05


def owners(positions, starts):
    inside = (positions[:, None] >= starts[None, :]) & (positions[:, None] < starts[None, :] + PIC)
    return jnp.max(jnp.where(inside, starts[None, :], -1), axis=1)


def visible_mask(query_pos, query_owner, key_pos, key_owner):
    later = key_pos[None, :] <= query_pos[:, None]
    shared = (key_owner[None, :] == query_owner[:, None]) & (query_owner[:, None] >= 0)
    return later | shared


def normalize(values):
    centre = values - jnp.mean(values, axis=-1, keepdims=True)
    inverse = lax.rsqrt(jnp.mean(centre * centre, axis=-1, keepdims=True) + EPS)
    return (centre * inverse, inverse)


def norm_back(upstream, normed, inverse, gain):
    scaled = upstream * gain
    return inverse * (
        scaled
        - jnp.mean(scaled, axis=-1, keepdims=True)
        - normed * jnp.mean(scaled * normed, axis=-1, keepdims=True)
    )


def matmul(left, right):
    return jnp.dot(left, right, preferred_element_type=jnp.float32)


def left_trans(left, right):
    return lax.dot_general(
        left, right, (((0,), (0,)), ((), ())), preferred_element_type=jnp.float32
    )


def right_trans(left, right):
    return lax.dot_general(
        left, right, (((1,), (1,)), ((), ())), preferred_element_type=jnp.float32
    )


def key_blocks(count):
    size = math.gcd(count, 1024)
    return (size, count // size)


def gather_forward(shards):
    return (
        lax.all_gather(shards[0], ("dp", "seq"), axis=0, tiled=True),
        lax.all_gather(shards[1], ("dp", "seq"), axis=0, tiled=True),
        lax.all_gather(shards[2], ("dp", "seq"), axis=0, tiled=True),
        lax.all_gather(shards[3], ("dp", "seq"), axis=0, tiled=True),
        lax.all_gather(shards[4], ("dp", "seq"), axis=0, tiled=True),
        lax.all_gather(shards[5], ("dp", "seq"), axis=0, tiled=True),
        lax.all_gather(shards[6], ("dp", "seq"), axis=0, tiled=True),
        lax.all_gather(shards[7], ("dp", "seq"), axis=0, tiled=True),
        lax.all_gather(shards[8], ("dp", "seq"), axis=0, tiled=True),
        lax.all_gather(shards[9], ("dp", "seq"), axis=0, tiled=True),
        lax.all_gather(shards[10], ("dp", "seq"), axis=0, tiled=True),
        lax.all_gather(shards[11], ("dp", "seq"), axis=0, tiled=True),
    )


def gather_backward(shards):
    return (
        lax.all_gather(shards[0], ("dp", "seq"), axis=0, tiled=True),
        lax.all_gather(shards[1], ("dp", "seq"), axis=0, tiled=True),
        lax.all_gather(shards[2], ("dp", "seq"), axis=0, tiled=True),
        lax.all_gather(shards[3], ("dp", "seq"), axis=0, tiled=True),
        lax.all_gather(shards[4], ("dp", "seq"), axis=0, tiled=True),
        lax.all_gather(shards[5], ("dp", "seq"), axis=0, tiled=True),
        lax.all_gather(shards[6], ("dp", "seq"), axis=0, tiled=True),
        lax.all_gather(shards[7], ("dp", "seq"), axis=0, tiled=True),
        lax.all_gather(shards[8], ("dp", "seq"), axis=0, tiled=True),
        lax.all_gather(shards[9], ("dp", "seq"), axis=0, tiled=True),
        lax.all_gather(shards[10], ("dp", "seq"), axis=0, tiled=True),
        lax.all_gather(shards[11], ("dp", "seq"), axis=0, tiled=True),
    )


def column_sum(values):
    return jnp.sum(values.astype(jnp.float32), axis=0)


def on_device(
    tokens,
    piece_starts,
    qkv_weight,
    qv_bias,
    out_weight,
    out_bias,
    norm1_gain,
    norm1_bias,
    up_weight,
    up_bias,
    down_weight,
    down_bias,
    norm2_gain,
    norm2_bias,
    grad_out,
):
    shards = (
        qkv_weight,
        qv_bias,
        out_weight,
        out_bias,
        norm1_gain,
        norm1_bias,
        up_weight,
        up_bias,
        down_weight,
        down_bias,
        norm2_gain,
        norm2_bias,
    )
    micro_count = tokens.shape[0]
    rows = tokens.shape[2]
    width = tokens.shape[3]
    head_size = width // HEADS
    scale = 1.0 / math.sqrt(head_size)
    length = rows * lax.axis_size("seq")
    query_pos = lax.axis_index("seq") * rows + jnp.arange(rows, dtype=jnp.int32)
    totals = None
    outputs = []
    input_grads = []
    for micro in range(micro_count):
        params = gather_forward(shards)
        (
            full_qkv,
            full_qvb,
            full_out,
            full_outb,
            full_g1,
            full_b1,
            full_up,
            full_upb,
            full_down,
            full_downb,
            full_g2,
            full_b2,
        ) = params
        starts = piece_starts[micro, 0]
        query_owner = owners(query_pos, starts)
        source = tokens[micro, 0]
        joined = matmul(source, full_qkv)
        queries = (joined[:, :width] + full_qvb[:width].astype(jnp.float32)).astype(jnp.bfloat16)
        keys = joined[:, width : 2 * width].astype(jnp.bfloat16)
        values = (joined[:, 2 * width :] + full_qvb[width:].astype(jnp.float32)).astype(
            jnp.bfloat16
        )
        query_heads = queries.reshape(rows, HEADS, head_size)

        def block_scores(key_block, key_pos):
            scores = (
                jnp.einsum(
                    "qhd,khd->hqk", query_heads, key_block, preferred_element_type=jnp.float32
                )
                * scale
            )
            allowed = visible_mask(query_pos, query_owner, key_pos, owners(key_pos, starts))
            return jnp.where(allowed[None], scores, NEG)

        initial = (
            jnp.full((HEADS, rows), NEG, jnp.float32),
            jnp.zeros((HEADS, rows), jnp.float32),
            jnp.zeros((HEADS, rows, head_size), jnp.float32),
        )
        key_piece = lax.all_gather(keys, "seq", axis=0, tiled=True)
        value_piece = lax.all_gather(values, "seq", axis=0, tiled=True)
        size, count = key_blocks(key_piece.shape[0])

        def one(block, carry):
            run_max, total, accum = carry
            key_block = lax.dynamic_slice_in_dim(key_piece, block * size, size, 0).reshape(
                size, HEADS, head_size
            )
            value_block = lax.dynamic_slice_in_dim(value_piece, block * size, size, 0).reshape(
                size, HEADS, head_size
            )
            key_pos = block * size + jnp.arange(size, dtype=jnp.int32)
            scores = block_scores(key_block, key_pos)
            new_max = jnp.maximum(run_max, jnp.max(scores, axis=-1))
            factor = jnp.exp(run_max - new_max)
            weights = jnp.exp(scores - new_max[:, :, None])
            total = total * factor + jnp.sum(weights, axis=-1)
            accum = accum * factor[:, :, None] + jnp.einsum(
                "hqk,khd->hqd",
                weights.astype(jnp.bfloat16),
                value_block,
                preferred_element_type=jnp.float32,
            )
            return (new_max, total, accum)

        run_max, total, accum = lax.fori_loop(0, count, one, initial)
        lse = run_max + jnp.log(total)
        exact = (accum / total[:, :, None]).transpose(1, 0, 2)
        attended = exact.reshape(rows, width).astype(jnp.bfloat16)
        resid1 = (
            source.astype(jnp.float32) + matmul(attended, full_out) + full_outb.astype(jnp.float32)
        )
        normed1, inverse1 = normalize(resid1)
        gain1 = full_g1.astype(jnp.float32)
        mixed1 = normed1 * gain1 + full_b1.astype(jnp.float32)
        inner = mixed1.astype(jnp.bfloat16)
        pre = matmul(inner, full_up) + full_upb.astype(jnp.float32)
        act = jax.nn.gelu(pre, approximate=False).astype(jnp.bfloat16)
        resid2 = mixed1 + matmul(act, full_down) + full_downb.astype(jnp.float32)
        normed2, inverse2 = normalize(resid2)
        gain2 = full_g2.astype(jnp.float32)
        outputs.append((normed2 * gain2 + full_b2.astype(jnp.float32)).astype(jnp.bfloat16))
        back = gather_backward(shards)
        back_qkv = back[0]
        back_out = back[2]
        back_up = back[6]
        back_down = back[8]
        cotan = grad_out[micro, 0].astype(jnp.float32)
        d_resid2 = norm_back(cotan, normed2, inverse2, gain2)
        grad_g2 = jnp.sum(cotan * normed2, axis=0)
        grad_b2 = jnp.sum(cotan, axis=0)
        d_branch2 = d_resid2.astype(jnp.bfloat16)
        grad_downb = column_sum(d_branch2)
        grad_down = left_trans(act, d_branch2)
        d_act = right_trans(d_branch2, back_down)
        gelu_value, gelu_back = jax.vjp(lambda value: jax.nn.gelu(value, approximate=False), pre)
        d_pre = gelu_back(d_act)[0].astype(jnp.bfloat16)
        grad_upb = column_sum(d_pre)
        grad_up = left_trans(inner, d_pre)
        d_mixed1 = d_resid2 + right_trans(d_pre, back_up)
        d_resid1 = norm_back(d_mixed1, normed1, inverse1, gain1)
        grad_g1 = jnp.sum(d_mixed1 * normed1, axis=0)
        grad_b1 = jnp.sum(d_mixed1, axis=0)
        d_branch1 = d_resid1.astype(jnp.bfloat16)
        grad_outb = column_sum(d_branch1)
        grad_out_w = left_trans(attended, d_branch1)
        d_attended = right_trans(d_branch1, back_out).astype(jnp.bfloat16)
        grad_heads = d_attended.reshape(rows, HEADS, head_size)
        delta = jnp.sum(grad_heads.astype(jnp.float32) * exact, axis=-1).T
        initial_back = (
            jnp.zeros((rows, HEADS, head_size), jnp.float32),
            jnp.zeros((length, width), jnp.float32),
            jnp.zeros((length, width), jnp.float32),
        )
        fold_key_piece = lax.all_gather(keys, "seq", axis=0, tiled=True)
        fold_value_piece = lax.all_gather(values, "seq", axis=0, tiled=True)
        fold_size, fold_count = key_blocks(fold_key_piece.shape[0])

        def fold_one(block, carry):
            query_grad, key_grads, value_grads = carry
            offset = block * fold_size
            key_block = lax.dynamic_slice_in_dim(fold_key_piece, offset, fold_size, 0).reshape(
                fold_size, HEADS, head_size
            )
            value_block = lax.dynamic_slice_in_dim(fold_value_piece, offset, fold_size, 0).reshape(
                fold_size, HEADS, head_size
            )
            key_pos = offset + jnp.arange(fold_size, dtype=jnp.int32)
            probs = jnp.exp(block_scores(key_block, key_pos) - lse[:, :, None])
            d_probs = jnp.einsum(
                "qhd,khd->hqk", grad_heads, value_block, preferred_element_type=jnp.float32
            )
            d_scores = (probs * (d_probs - delta[:, :, None])).astype(jnp.bfloat16)
            query_grad = (
                query_grad
                + jnp.einsum(
                    "hqk,khd->qhd", d_scores, key_block, preferred_element_type=jnp.float32
                )
                * scale
            )
            key_part = (
                jnp.einsum(
                    "hqk,qhd->khd", d_scores, query_heads, preferred_element_type=jnp.float32
                ).reshape(fold_size, width)
                * scale
            )
            value_part = jnp.einsum(
                "hqk,qhd->khd",
                probs.astype(jnp.bfloat16),
                grad_heads,
                preferred_element_type=jnp.float32,
            ).reshape(fold_size, width)
            key_grads = lax.dynamic_update_slice_in_dim(
                key_grads,
                lax.dynamic_slice_in_dim(key_grads, offset, fold_size, 0) + key_part,
                offset,
                0,
            )
            value_grads = lax.dynamic_update_slice_in_dim(
                value_grads,
                lax.dynamic_slice_in_dim(value_grads, offset, fold_size, 0) + value_part,
                offset,
                0,
            )
            return (query_grad, key_grads, value_grads)

        query_grad, key_grads, value_grads = lax.fori_loop(0, fold_count, fold_one, initial_back)
        key_grad, value_grad = (
            lax.psum_scatter(
                key_grads.astype(jnp.bfloat16), "seq", scatter_dimension=0, tiled=True
            ).astype(jnp.float32),
            lax.psum_scatter(
                value_grads.astype(jnp.bfloat16), "seq", scatter_dimension=0, tiled=True
            ).astype(jnp.float32),
        )
        query_share = query_grad.reshape(rows, width)
        d_queries = query_share.astype(jnp.bfloat16)
        d_keys = key_grad.astype(jnp.bfloat16)
        d_values = value_grad.astype(jnp.bfloat16)
        d_joined = jnp.concatenate([d_queries, d_keys, d_values], axis=1)
        grad_qvb = jnp.concatenate([column_sum(d_queries), column_sum(d_values)], axis=0)
        grad_qkv = left_trans(source, d_joined)
        input_grads.append(d_resid1 + right_trans(d_joined, back_qkv))
        terms = (
            grad_qkv,
            grad_qvb,
            grad_out_w,
            grad_outb,
            grad_g1,
            grad_b1,
            grad_up,
            grad_upb,
            grad_down,
            grad_downb,
            grad_g2,
            grad_b2,
        )
        if totals is None:
            totals = terms
        else:
            totals = tuple((first + second for first, second in zip(totals, terms)))
    shares = lax.psum_scatter(totals, ("dp", "seq"), scatter_dimension=0, tiled=True)
    layer_out = jnp.stack(outputs)[:, None]
    tokens_grad = jnp.stack(input_grads)[:, None]
    return (
        layer_out,
        tokens_grad,
        shares[0],
        shares[1],
        shares[2],
        shares[3],
        shares[4],
        shares[5],
        shares[6],
        shares[7],
        shares[8],
        shares[9],
        shares[10],
        shares[11],
    )


def solution(mesh):
    return jax.shard_map(
        on_device,
        mesh=mesh,
        in_specs=(
            P(None, "dp", "seq", None),
            P(None, "dp", None),
            P(("dp", "seq"), None),
            P(("dp", "seq")),
            P(("dp", "seq"), None),
            P(("dp", "seq")),
            P(("dp", "seq")),
            P(("dp", "seq")),
            P(("dp", "seq"), None),
            P(("dp", "seq")),
            P(("dp", "seq"), None),
            P(("dp", "seq")),
            P(("dp", "seq")),
            P(("dp", "seq")),
            P(None, "dp", "seq", None),
        ),
        out_specs=(
            P(None, "dp", "seq", None),
            P(None, "dp", "seq", None),
            P(("dp", "seq"), None),
            P(("dp", "seq")),
            P(("dp", "seq"), None),
            P(("dp", "seq")),
            P(("dp", "seq")),
            P(("dp", "seq")),
            P(("dp", "seq"), None),
            P(("dp", "seq")),
            P(("dp", "seq"), None),
            P(("dp", "seq")),
            P(("dp", "seq")),
            P(("dp", "seq")),
        ),
        check_vma=False,
    )
```

profile of v0, /device:TPU:0, one launch (start us, length us, event | category | flops | bytes accessed | tf_op | source)
XLA Modules:
  0.0 927.6 jit_solution(920579388821818816)
XLA Ops:
  16.8 42.6 %all-reduce.17 = (bf16[3072]{0:T(1024)(128)(2,1)S(1)}, bf16[1536]{0:T(1024)(128)(2,1)S(1)}, bf16[768]{0:T(1024)(128)(2,1)S(1)}, bf16[768]{0:T(1024)(128)(2,1)S(1...) all-reduce(bf16[3072]{0:T(1024)(128)(2,1)S(1)} %dynamic-update-slic, ...), channel_id=1, replica_groups=mesh['dp'=8,'seq'=4] {'dp','seq'}, use_global_device_ids=true, to_apply=%add.4 | all-reduce | flops 9216 | bytes 36864
  64.7 8.9 all-gather.5.cloned.1.call-done
  73.6 2.9 fusion.95
  77.7 12.7 %all_gather.34 = bf16[512,768]{1,0:T(8,128)(2,1)S(1)} all-gather(bf16[128,768]{1,0:T(8,128)(2,1)S(1)} %slice.119), channel_id=1, replica_groups=mesh['dp'=8,'seq'=4] {'seq'}, dimensions={0}, use_global_device_ids=true | all-gather | bytes 983040 | tf_op jit(solution)/shard_map/all_gather | solution.py:181
  91.6 10.5 %all_gather.35 = bf16[512,768]{1,0:T(8,128)(2,1)S(1)} all-gather(bf16[128,768]{1,0:T(8,128)(2,1)S(1)} %get-tuple-element.277), channel_id=1, replica_groups=mesh['dp'=8,'seq'=4] {'seq'}, dimensions={0}, use_global_device_ids=true | all-gather | bytes 983040 | tf_op jit(solution)/shard_map/all_gather | solution.py:182
  104.0 12.6 %all_gather.86 = bf16[512,768]{1,0:T(8,128)(2,1)S(1)} all-gather(bf16[128,768]{1,0:T(8,128)(2,1)S(1)} %slice.118), channel_id=1, replica_groups=mesh['dp'=8,'seq'=4] {'seq'}, dimensions={0}, use_global_device_ids=true | all-gather | bytes 983040 | tf_op jit(solution)/shard_map/all_gather | solution.py:181
  117.8 10.7 %all_gather.87 = bf16[512,768]{1,0:T(8,128)(2,1)S(1)} all-gather(bf16[128,768]{1,0:T(8,128)(2,1)S(1)} %get-tuple-element.271), channel_id=1, replica_groups=mesh['dp'=8,'seq'=4] {'seq'}, dimensions={0}, use_global_device_ids=true | all-gather | bytes 983040 | tf_op jit(solution)/shard_map/all_gather | solution.py:182
  129.7 1.9 fusion.136
  132.7 1.6 fusion.137
  134.3 1.9 fusion.138
  139.2 1.5 fusion.141
  143.2 52.6 %all-gather.9.cloned.1.call-done = bf16[768,3072]{1,0:T(8,128)(2,1)} async-done(((bf16[24,3072]{1,0:T(8,128)(2,1)}), bf16[768,3072]{1,0:T(8,128)(2,1)}) %all-gather.9.cloned.1.call-update) | async-done | bytes 4718608 | tf_op jit(solution)/shard_map/all_gather | solution.py:68
  195.8 8.7 multiply_convert_fusion.5
  204.5 55.9 %all-gather.11.cloned.1.call-done = bf16[3072,768]{1,0:T(8,128)(2,1)} async-done(((bf16[96,768]{1,0:T(8,128)(2,1)}), bf16[3072,768]{1,0:T(8,128)(2,1)}) %all-gather.11.cloned.1.call-update) | async-done | bytes 4718608 | tf_op jit(solution)/shard_map/all_gather | solution.py:70
  260.4 3.6 fusion.139
  264.5 5.5 multiply_convert_fusion.4
  272.3 1.7 convert_reduce_fusion.4
  274.0 2.5 convert_reduce_fusion.1
  276.5 2.4 multiply_reduce_fusion.1
  278.8 2.5 convert_reduce_fusion
  281.3 3.1 convert_reduce_fusion.7
  287.4 1.7 copy.75
  289.1 3.6 fusion.33
  292.7 2.4 copy.85
  296.2 3.1 multiply_convert_fusion
  301.8 2.3 copy.83
  304.1 2.7 convolution_convert_fusion.1
  306.8 1.7 copy.74
  308.5 2.6 fusion.30
  311.1 2.3 copy.81
  314.6 2.2 multiply_convert_fusion.1
  320.6 1.9 convolution_add_fusion.4
  323.9 2.5 convert_reduce_fusion.9
  328.9 19.7 %reduce-scatter.29.cloned.1.call-done = bf16[128,768]{1,0:T(8,128)(2,1)} async-done(((bf16[512,768]{1,0:T(8,128)(2,1)}), bf16[128,768]{1,0:T(8,128)(2,1)}) %reduce-scatter.29.cloned.1.call-update) | async-done | bytes 196624
  349.7 28.0 %reduce-scatter.27.cloned.1.call-done = bf16[128,768]{1,0:T(8,128)(2,1)} async-done(((bf16[512,768]{1,0:T(8,128)(2,1)}), bf16[128,768]{1,0:T(8,128)(2,1)}) %reduce-scatter.27.cloned.1.call-update) | async-done | bytes 196624
  378.8 28.0 %reduce-scatter.25.cloned.1.call-done = bf16[128,768]{1,0:T(8,128)(2,1)} async-done(((bf16[512,768]{1,0:T(8,128)(2,1)}), bf16[128,768]{1,0:T(8,128)(2,1)}) %reduce-scatter.25.cloned.1.call-update) | async-done | bytes 196624
  409.0 4.0 add_bitcast_fusion
  413.0 8.0 copy.87
  422.2 1.5 fusion.129
  423.7 5.1 convolution_add_fusion.1
  431.6 5.1 convolution_add_fusion
  446.4 1.8 maximum_bitcast_fusion.1
  451.6 41.7 %all-reduce.16 = (f32[1536]{0:T(1024)}, f32[768]{0:T(1024)}, f32[768]{0:T(1024)}, f32[768]{0:T(1024)}, f32[3072]{0:T(1024)}, /*index=5*/f32[768]{0:T(1024)}, f32[768]{0:T(1024)}, f32[768]{0:T(1024)}) all-reduce(f32[1536]{0:T(1024)} %maximum_add_fusion, f32[768]{0:T(1024)S(1)} %add.424, ...), channel_id=7, replica_groups=mesh['dp'=8,'seq'=4] {'dp','seq'}, use_global_device_ids=true, to_apply=%region_35.36.clone | all-reduce | flops 9216 | bytes 73728
  503.5 2.6 fusion.56
  508.4 4.1 reduce-scatter.19.cloned.1.call-done
  512.5 124.8 %reduce-scatter.33.cloned.1.call-done = f32[24,2304]{1,0:T(8,128)} async-done(((f32[768,2304]{1,0:T(8,128)}), f32[24,2304]{1,0:T(8,128)}) %reduce-scatter.33.cloned.1.call-update) | async-done | bytes 221200
  637.3 141.6 %reduce-scatter.21.cloned.1.call-done = f32[24,3072]{1,0:T(8,128)} async-done(((f32[768,3072]{1,0:T(8,128)}), f32[24,3072]{1,0:T(8,128)}) %reduce-scatter.21.cloned.1.call-update) | async-done | bytes 294928 | tf_op jit(solution)/shard_map/reduce_scatter | solution.py:343
  778.9 141.5 %reduce-scatter.23.cloned.1.call-done = f32[96,768]{1,0:T(8,128)} async-done(((f32[3072,768]{1,0:T(8,128)}), f32[96,768]{1,0:T(8,128)}) %reduce-scatter.23.cloned.1.call-update) | async-done | bytes 294928 | tf_op jit(solution)/shard_map/reduce_scatter | solution.py:343
  (282 shorter events, 79.6 us)
Async XLA Ops:
  7.2 66.4 %all-gather.5.cloned.1.call-start = ((), (), s32[]{:S(2)}) async-start(), calls=%async_computation.8 | async-start | bytes 3649536 | tf_op jit(solution)/shard_map/all_gather | solution.py:62
  7.9 126.4 %all-gather.7.cloned.1.call-start = ((), (), s32[]{:S(2)}) async-start(), calls=%async_computation.9 | async-start | bytes 1216512 | tf_op jit(solution)/shard_map/all_gather | solution.py:64
  8.7 187.2 %all-gather.9.cloned.1.call-start = ((), (), s32[]{:S(2)}) async-start(), calls=%async_computation.10 | async-start | bytes 4866048 | tf_op jit(solution)/shard_map/all_gather | solution.py:68
  9.4 251.0 %all-gather.11.cloned.1.call-start = ((), (), s32[]{:S(2)}) async-start(), calls=%async_computation.11 | async-start | bytes 4866048 | tf_op jit(solution)/shard_map/all_gather | solution.py:70
  10.0 317.8 %reduce-scatter.31.cloned.1.call-start = ((), (), s32[]{:S(2)}) async-start(), calls=%async_computation.18 | async-start | bytes 983040
  64.7 11.9 %copy-start.22 = (bf16[2,1,128,768]{3,2,1,0:T(8,128)(2,1)S(1)}, bf16[2,1,128,768]{3,2,1,0:T(8,128)(2,1)}, u32[]{:S(2)}) copy-start(bf16[2,1,128,768]{3,2,1,0:T(8,128)(2,1)} %param.15) | copy-start | bytes 1179652
  73.6 3.2 copy-start.1
  77.7 52.0 %copy-start.42 = (bf16[128,768]{0,1:T(8,128)(2,1)}, bf16[128,768]{0,1:T(8,128)(2,1)S(1)}, u32[]{:S(2)}) copy-start(bf16[128,768]{0,1:T(8,128)(2,1)S(1)} %copy.68) | copy-start | bytes 589828
  260.4 4.0 copy-start.3
  260.4 9.6 %slice-start = ((s8[4718592]{0:T(1024)(128)(4,1)}), s8[4194304]{0:T(1024)(128)(4,1)S(1)}, s32[]{:S(2)}) async-start(s8[4718592]{0:T(1024)(128)(4,1)} %bitcast.187), calls=%async_computation.20 | async-start | bytes 8388608
  264.4 5.6 slice-start.1
  264.4 5.6 copy-start.11
  264.4 5.6 copy-start.54
  264.4 5.6 copy-start.62
  264.5 5.6 copy-start.66
  271.3 2.7 copy-start.68
  271.3 2.7 copy-start.69
  274.0 2.5 copy-start.27
  274.0 7.3 copy-start.25
  274.0 2.5 copy-start.58
  281.3 3.1 copy-start.33
  295.1 53.6 %reduce-scatter.29.cloned.1.call-start = ((), (), s32[]{:S(2)}) async-start(), calls=%async_computation.17 | async-start | bytes 983040
  296.2 4.3 copy-start.45
  304.1 73.6 %reduce-scatter.27.cloned.1.call-start = ((), (), s32[]{:S(2)}) async-start(), calls=%async_computation.16 | async-start | bytes 983040
  313.4 93.4 %reduce-scatter.25.cloned.1.call-start = ((), (), s32[]{:S(2)}) async-start(), calls=%async_computation.15 | async-start | bytes 983040
  314.6 3.3 copy-start.43
  319.6 193.0 %reduce-scatter.19.cloned.1.call-start = ((), (), s32[]{:S(2)}) async-start(), calls=%async_computation.12 | async-start | bytes 2433024 | tf_op jit(solution)/shard_map/reduce_scatter | solution.py:343
  322.5 3.9 copy-start.9
  322.5 314.8 %reduce-scatter.33.cloned.1.call-start = ((), (), s32[]{:S(2)}) async-start(), calls=%async_computation.19 | async-start | bytes 7299072
  323.9 2.5 copy-start.13
  326.4 81.5 %copy-start.24 = (bf16[2,1,128,768]{3,2,1,0:T(8,128)(2,1)S(1)}, bf16[2,1,128,768]{3,2,1,0:T(8,128)(2,1)}, u32[]{:S(2)}) copy-start(bf16[2,1,128,768]{3,2,1,0:T(8,128)(2,1)} %param.15) | copy-start | bytes 1179652
  327.8 81.2 %copy-start.48 = (bf16[12,64,128]{2,1,0:T(8,128)(2,1)}, bf16[12,64,128]{2,1,0:T(8,128)(2,1)S(1)}, u32[]{:S(2)}) copy-start(bf16[12,64,128]{2,1,0:T(8,128)(2,1)S(1)} %get-tuple-element.316) | copy-start | bytes 589828
  328.9 80.1 %copy-start.30 = (bf16[128,768]{0,1:T(8,128)(2,1)}, bf16[128,768]{0,1:T(8,128)(2,1)S(1)}, u32[]{:S(2)}) copy-start(bf16[128,768]{0,1:T(8,128)(2,1)S(1)} %copy.86) | copy-start | bytes 589828
  349.7 59.3 %copy-start.40 = (bf16[128,768]{0,1:T(8,128)(2,1)}, bf16[128,768]{0,1:T(8,128)(2,1)S(1)}, u32[]{:S(2)}) copy-start(bf16[128,768]{0,1:T(8,128)(2,1)S(1)} %copy.84) | copy-start | bytes 589828
  378.8 30.2 %copy-start.35 = (bf16[128,768]{0,1:T(8,128)(2,1)}, bf16[128,768]{0,1:T(8,128)(2,1)S(1)}, u32[]{:S(2)}) copy-start(bf16[128,768]{0,1:T(8,128)(2,1)S(1)} %copy.82) | copy-start | bytes 589828
  421.1 2.6 copy-start.12
  421.1 2.6 copy-start.34
  421.1 2.6 copy-start.63
  421.1 2.6 copy-start.67
  421.1 357.8 %reduce-scatter.21.cloned.1.call-start = ((), (), s32[]{:S(2)}) async-start(), calls=%async_computation.13 | async-start | bytes 9732096 | tf_op jit(solution)/shard_map/reduce_scatter | solution.py:343
  428.9 2.6 copy-start.26
  428.9 2.6 copy-start.32
  428.9 491.4 %reduce-scatter.23.cloned.1.call-start = ((), (), s32[]{:S(2)}) async-start(), calls=%async_computation.14 | async-start | bytes 9732096 | tf_op jit(solution)/shard_map/reduce_scatter | solution.py:343
  436.7 66.8 %copy-start.2 = (bf16[768,2304]{1,0:T(8,128)(2,1)S(1)}, bf16[768,2304]{1,0:T(8,128)(2,1)}, u32[]{:S(2)}) copy-start(bf16[768,2304]{1,0:T(8,128)(2,1)} %all-gather.5.cloned.1.call-done) | copy-start | bytes 10616836
  503.5 2.7 copy-start.18
  503.5 2.7 copy-start.36
  503.5 2.7 copy-start.49
  503.5 2.7 copy-start.51
  (36 other events, 50.8 us)
Sparse Core Ops, SparseCore 0:
  10.9 62.6 all-gather.4
  76.5 53.7 all-gather.6
  133.1 62.6 all-gather.8
  198.6 61.8 all-gather.10
  295.2 24.4 reduce-scatter.30
  322.4 26.1 reduce-scatter.28
  351.5 26.1 reduce-scatter.26
  380.6 26.1 reduce-scatter.24
  412.7 99.7 reduce-scatter.18
  518.6 118.6 reduce-scatter.32
  643.8 135.0 reduce-scatter.20
  785.2 135.1 reduce-scatter.22
where the time goes:
time: 934 us; the launch traced here: 928 us
  waiting for transfers between devices  608 us (65%)
  blocking collectives  131 us (14%)
  matrix products  86 us (9%)
  local copies, waits for them, and re-layouts  57.4 us (6%)
  other arithmetic  29.5 us (3%)
  between operations  15.5 us (2%)
    reduce_scatter x3, waiting for transfers between devices, on_device(): lax.psum_scatter(totals, ('dp', 'seq'), scatter_dimension=0, tiled=True)  287 us
    unnamed x17, waiting for transfers between devices  203 us
    unnamed x2, blocking collectives  84.3 us
    all_gather x1, waiting for transfers between devices, gather_forward(): lax.all_gather(shards[8], ('dp', 'seq'), axis=0, tiled=True)  55.9 us
    all_gather x1, waiting for transfers between devices, gather_forward(): lax.all_gather(shards[6], ('dp', 'seq'), axis=0, tiled=True)  52.6 us
    unnamed x177, local copies, waits for them, and re-layouts  46.3 us
    all_gather x2, blocking collectives, on_device(): key_piece = lax.all_gather(keys, 'seq', axis=0, tiled=True)  25.3 us
    dot_general x8, matrix products, matmul(): return jnp.dot(left, right, preferred_element_type=jnp.float32)  24.6 us
  transfers between devices with their start and end apart: 12, of which 10 were waited for; matrix products, arithmetic and copies ran while one was open for 14% of the time, Pallas kernels for 0%

commit v1 on v0

--- a/solution.py
+++ b/solution.py
@@ -178,8 +178,16 @@
             jnp.zeros((HEADS, rows), jnp.float32),
             jnp.zeros((HEADS, rows, head_size), jnp.float32),
         )
-        key_piece = lax.all_gather(keys, "seq", axis=0, tiled=True)
-        value_piece = lax.all_gather(values, "seq", axis=0, tiled=True)
+
+        def plate_measure(matrix, sheet):
+            oldest = jnp.split(
+                lax.all_gather(jnp.concatenate([matrix, sheet], axis=1), "seq", axis=0, tiled=True),
+                [matrix.shape[1]],
+                axis=1,
+            )
+            return oldest
+
+        key_piece, value_piece = plate_measure(keys, values)
         size, count = key_blocks(key_piece.shape[0])
 
         def one(block, carry):

time: 934 us -> 1020 us (1.092)
  local copies, waits for them, and re-layouts: 57.4 us -> 83.4 us
  waiting for transfers between devices: 608 us -> 629 us
  matrix products: 86 us -> 104 us
  blocking collectives: 131 us -> 147 us
    unnamed x17 -> x19, waiting for transfers between devices: 203 us -> 147 us
    all_gather x1, waiting for transfers between devices: 0.01 us -> 46.5 us  [gather_forward(): lax.all_gather(shards[2], ('dp', 'seq'), axis=0, tiled=True)]
    all_gather x0 -> x2, waiting for transfers between devices: none -> 19.6 us  [plate_measure(): lax.all_gather(jnp.concatenate([matrix, sheet], axis=1), 'seq', axis=0, t...]
    all_gather x4, blocking collectives: 46.5 us -> 62.6 us  [the longest x2 33.6 us: on_device(): fold_key_piece = lax.all_gather(keys, 'seq', axis=0, tiled=True)]
    split x0 -> x6, local copies, waits for them, and re-layouts: none -> 14.5 us  [plate_measure(): jnp.split(lax.all_gather(jnp.concatenate([matrix, sheet], axis=1), 'seq',...]
    unnamed x177 -> x179, local copies, waits for them, and re-layouts: 46.3 us -> 49.6 us
  transfers between devices with their start and end apart: 12 -> 14, of which waited for: 10 -> 10; matrix products, arithmetic and copies ran while one was open for 14% -> 17% of each run, Pallas kernels for 0% -> 0%
where the time goes in v1:
time: 1020 us; the launch traced here: 1010 us
  waiting for transfers between devices  629 us (62%)
  blocking collectives  147 us (14%)
  matrix products  104 us (10%)
  local copies, waits for them, and re-layouts  83.4 us (8%)
  other arithmetic  35.6 us (3%)
  between operations  15.1 us (1%)
    reduce_scatter x3, waiting for transfers between devices, on_device(): lax.psum_scatter(totals, ('dp', 'seq'), scatter_dimension=0, tiled=True)  285 us
    unnamed x19, waiting for transfers between devices  147 us
    unnamed x2, blocking collectives  84.4 us
    all_gather x1, waiting for transfers between devices, gather_forward(): lax.all_gather(shards[6], ('dp', 'seq'), axis=0, tiled=True)  58.1 us
    all_gather x1, waiting for transfers between devices, gather_forward(): lax.all_gather(shards[8], ('dp', 'seq'), axis=0, tiled=True)  56.2 us
    unnamed x179, local copies, waits for them, and re-layouts  49.6 us
    all_gather x1, waiting for transfers between devices, gather_forward(): lax.all_gather(shards[2], ('dp', 'seq'), axis=0, tiled=True)  46.5 us
    all_gather x2, blocking collectives, on_device(): fold_key_piece = lax.all_gather(keys, 'seq', axis=0, tiled=True)  33.6 us
  transfers between devices with their start and end apart: 14, of which 10 were waited for; matrix products, arithmetic and copies ran while one was open for 17% of the time, Pallas kernels for 0%

profile of v1, /device:TPU:0, one launch (start us, length us, event | category | flops | bytes accessed | tf_op | source)
XLA Modules:
  0.0 1014.5 jit_solution(15896169749843315307)
XLA Ops:
  14.7 42.8 %all-reduce.17 = (bf16[3072]{0:T(1024)(128)(2,1)}, bf16[1536]{0:T(1024)(128)(2,1)S(1)}, bf16[768]{0:T(1024)(128)(2,1)}, bf16[768]{0:T(1024)(128)(2,1)}, bf16[768...) all-reduce(bf16[3072]{0:T(1024)(128)(2,1)S(1)} %dynamic-update-slic, ...), channel_id=1, replica_groups=mesh['dp'=8,'seq'=4] {'dp','seq'}, use_global_device_ids=true, to_apply=%add.4 | all-reduce | flops 9216 | bytes 36864
  57.5 16.2 %all-gather.7.cloned.1.call-done = bf16[768,2304]{1,0:T(8,128)(2,1)} async-done(((bf16[24,2304]{1,0:T(8,128)(2,1)}), bf16[768,2304]{1,0:T(8,128)(2,1)}) %all-gather.7.cloned.1.call-update) | async-done | bytes 3538960 | tf_op jit(solution)/shard_map/all_gather | solution.py:62
  73.7 2.9 fusion.109
  97.1 19.7 %all_gather.90 = bf16[512,768]{1,0:T(8,128)(2,1)} all-gather(bf16[128,768]{1,0:T(8,128)(2,1)} %copy-done.43), channel_id=1, replica_groups=mesh['dp'=8,'seq'=4] {'seq'}, dimensions={0}, use_global_device_ids=true | all-gather | bytes 983040 | tf_op jit(solution)/shard_map/all_gather | solution.py:264
  119.1 3.5 fusion.167
  122.6 2.6 fusion.158
  125.2 2.3 copy.81
  129.8 19.6 %all-gather.17.cloned.1.call-done = bf16[512,1536]{1,0:T(8,128)(2,1)} async-done(((bf16[128,1536]{1,0:T(8,128)(2,1)}), bf16[512,1536]{1,0:T(8,128)(2,1)}) %all-gather.17.cloned.1.call-update) | async-done | bytes 1572880 | tf_op jit(solution)/shard_map/all_gather | solution.py:184
  149.5 2.6 fusion.159
  152.1 2.3 copy.84
  159.8 46.5 %all-gather.11.cloned.1.call-done = bf16[768,768]{1,0:T(8,128)(2,1)} async-done(((bf16[24,768]{1,0:T(8,128)(2,1)}), bf16[768,768]{1,0:T(8,128)(2,1)}) %all-gather.11.cloned.1.call-update) | async-done | bytes 1179664 | tf_op jit(solution)/shard_map/all_gather | solution.py:64
  213.3 58.1 %all-gather.13.cloned.1.call-done = bf16[768,3072]{1,0:T(8,128)(2,1)} async-done(((bf16[24,3072]{1,0:T(8,128)(2,1)}), bf16[768,3072]{1,0:T(8,128)(2,1)}) %all-gather.13.cloned.1.call-update) | async-done | bytes 4718608 | tf_op jit(solution)/shard_map/all_gather | solution.py:68
  271.4 8.5 multiply_convert_fusion.5
  279.9 56.2 %all-gather.15.cloned.1.call-done = bf16[3072,768]{1,0:T(8,128)(2,1)} async-done(((bf16[96,768]{1,0:T(8,128)(2,1)}), bf16[3072,768]{1,0:T(8,128)(2,1)}) %all-gather.15.cloned.1.call-update) | async-done | bytes 4718608 | tf_op jit(solution)/shard_map/all_gather | solution.py:70
  336.1 3.5 fusion.162
  341.1 2.3 copy.85
  343.4 4.2 fusion.163
  348.5 4.2 multiply_convert_fusion.4
  356.8 2.5 convert_reduce_fusion.1
  359.3 2.4 multiply_reduce_fusion.1
  361.7 2.5 convert_reduce_fusion
  364.1 3.5 convert_reduce_fusion.7
  372.2 3.7 fusion.47
  375.9 2.4 copy.101
  378.4 16.3 %all_gather.91 = bf16[512,768]{1,0:T(8,128)(2,1)} all-gather(bf16[128,768]{1,0:T(8,128)(2,1)} %get-tuple-element.275), channel_id=1, replica_groups=mesh['dp'=8,'seq'=4] {'seq'}, dimensions={0}, use_global_device_ids=true | all-gather | bytes 983040 | tf_op jit(solution)/shard_map/all_gather | solution.py:265
  398.1 3.4 multiply_convert_fusion
  406.4 13.9 %all_gather.88 = bf16[512,768]{1,0:T(8,128)(2,1)} all-gather(bf16[128,768]{1,0:T(8,128)(2,1)} %copy-done.42), channel_id=1, replica_groups=mesh['dp'=8,'seq'=4] {'seq'}, dimensions={0}, use_global_device_ids=true | all-gather | bytes 983040 | tf_op jit(solution)/shard_map/all_gather | solution.py:264
  420.3 2.3 copy.86
  422.7 3.6 fusion.166
  429.3 3.9 fusion.44
  433.2 2.3 copy.97
  435.6 12.7 %all_gather.89 = bf16[512,768]{1,0:T(8,128)(2,1)} all-gather(bf16[128,768]{1,0:T(8,128)(2,1)} %copy-done.41), channel_id=1, replica_groups=mesh['dp'=8,'seq'=4] {'seq'}, dimensions={0}, use_global_device_ids=true | all-gather | bytes 983040 | tf_op jit(solution)/shard_map/all_gather | solution.py:265
  448.2 2.4 copy.88
  451.7 3.4 multiply_convert_fusion.1
  463.7 3.2 convert_reduce_fusion.9
  474.0 19.8 %reduce-scatter.25.cloned.1.call-done = bf16[128,768]{1,0:T(8,128)(2,1)} async-done(((bf16[512,768]{1,0:T(8,128)(2,1)}), bf16[128,768]{1,0:T(8,128)(2,1)}) %reduce-scatter.25.cloned.1.call-update) | async-done | bytes 196624
  495.5 2.4 fusion.102
  497.9 4.0 add_bitcast_fusion
  501.9 8.1 copy.103
  510.1 2.9 fusion.151
  513.0 5.1 convolution_add_fusion.1
  518.2 2.8 fusion.135
  521.0 5.1 convolution_add_fusion
  540.9 41.6 %all-reduce.16 = (f32[1536]{0:T(1024)}, f32[768]{0:T(1024)}, f32[768]{0:T(1024)}, f32[768]{0:T(1024)}, f32[3072]{0:T(1024)}, /*index=5*/f32[768]{0:T(1024)}, f32[768]{0:T(1024)}, f32[768]{0:T(1024)}) all-reduce(f32[1536]{0:T(1024)} %maximum_add_fusion, f32[768]{0:T(1024)S(1)} %add.424, ...), channel_id=7, replica_groups=mesh['dp'=8,'seq'=4] {'dp','seq'}, use_global_device_ids=true, to_apply=%region_35.36.clone | all-reduce | flops 9216 | bytes 73728
  592.7 2.6 fusion.58
  599.4 124.8 %reduce-scatter.33.cloned.1.call-done = f32[24,2304]{1,0:T(8,128)} async-done(((f32[768,2304]{1,0:T(8,128)}), f32[24,2304]{1,0:T(8,128)}) %reduce-scatter.33.cloned.1.call-update) | async-done | bytes 221200
  724.2 141.7 %reduce-scatter.21.cloned.1.call-done = f32[24,3072]{1,0:T(8,128)} async-done(((f32[768,3072]{1,0:T(8,128)}), f32[24,3072]{1,0:T(8,128)}) %reduce-scatter.21.cloned.1.call-update) | async-done | bytes 294928 | tf_op jit(solution)/shard_map/reduce_scatter | solution.py:351
  865.9 141.8 %reduce-scatter.23.cloned.1.call-done = f32[96,768]{1,0:T(8,128)} async-done(((f32[3072,768]{1,0:T(8,128)}), f32[96,768]{1,0:T(8,128)}) %reduce-scatter.23.cloned.1.call-update) | async-done | bytes 294928 | tf_op jit(solution)/shard_map/reduce_scatter | solution.py:351
  (301 shorter events, 114.4 us)
Async XLA Ops:
  7.2 66.5 %all-gather.7.cloned.1.call-start = ((), (), s32[]{:S(2)}) async-start(), calls=%async_computation.8 | async-start | bytes 3649536 | tf_op jit(solution)/shard_map/all_gather | solution.py:62
  7.9 114.7 %all-gather.9.cloned.1.call-start = ((), (), s32[]{:S(2)}) async-start(), calls=%async_computation.9 | async-start | bytes 1966080 | tf_op jit(solution)/shard_map/all_gather | solution.py:184
  73.7 3.2 copy-start
  73.7 3.2 copy-start.19
  79.4 7.4 copy-start.63
  80.9 68.6 %all-gather.17.cloned.1.call-start = ((), (), s32[]{:S(2)}) async-start(), calls=%async_computation.13 | async-start | bytes 1966080 | tf_op jit(solution)/shard_map/all_gather | solution.py:184
  84.4 121.9 %all-gather.11.cloned.1.call-start = ((), (), s32[]{:S(2)}) async-start(), calls=%async_computation.10 | async-start | bytes 1216512 | tf_op jit(solution)/shard_map/all_gather | solution.py:64
  85.0 186.4 %all-gather.13.cloned.1.call-start = ((), (), s32[]{:S(2)}) async-start(), calls=%async_computation.11 | async-start | bytes 4866048 | tf_op jit(solution)/shard_map/all_gather | solution.py:68
  85.5 250.5 %all-gather.15.cloned.1.call-start = ((), (), s32[]{:S(2)}) async-start(), calls=%async_computation.12 | async-start | bytes 4866048 | tf_op jit(solution)/shard_map/all_gather | solution.py:70
  86.1 382.6 %reduce-scatter.31.cloned.1.call-start = ((), (), s32[]{:S(2)}) async-start(), calls=%async_computation.20 | async-start | bytes 983040
  206.2 3.4 copy-start.32
  206.2 3.4 copy-start.34
  206.2 3.4 copy-start.48
  343.4 5.0 slice-start
  343.4 4.3 copy-start.1
  343.4 4.3 copy-start.20
  343.4 4.3 copy-start.49
  343.4 5.0 slice-start.1
  347.7 4.9 slice-start.2
  348.2 19.5 %copy-start.5 = (f32[128,768]{1,0:T(8,128)}, f32[128,768]{1,0:T(8,128)S(1)}, u32[]{:S(2)}) copy-start(f32[128,768]{1,0:T(8,128)S(1)} %get-tuple-element.313) | copy-start | bytes 1179652
  348.2 19.5 %copy-start.55 = (f32[128]{0:T(128)}, f32[128]{0:T(128)S(1)}, u32[]{:S(2)}) copy-start(f32[128]{0:T(128)S(1)} %broadcast_multiply_fusion.9) | copy-start | bytes 1540
  348.5 19.2 %copy-start.59 = (f32[128]{0:T(128)}, f32[128]{0:T(128)S(1)}, u32[]{:S(2)}) copy-start(f32[128]{0:T(128)S(1)} %add_rsqrt_fusion.1) | copy-start | bytes 1540
  348.5 4.2 slice-start.3
  354.1 2.7 copy-start.67
  354.1 2.7 copy-start.68
  356.8 7.3 copy-start.22
  364.1 3.5 copy-start.29
  367.7 4.5 copy-start.62
  378.3 92.2 %reduce-scatter.29.cloned.1.call-start = ((), (), s32[]{:S(2)}) async-start(), calls=%async_computation.19 | async-start | bytes 983040
  398.1 4.6 copy-start.33
  406.3 65.9 %reduce-scatter.27.cloned.1.call-start = ((), (), s32[]{:S(2)}) async-start(), calls=%async_computation.18 | async-start | bytes 983040
  422.7 3.7 copy-start.2
  422.7 3.7 copy-start.9
  426.3 3.0 copy-start.61
  435.5 58.2 %reduce-scatter.25.cloned.1.call-start = ((), (), s32[]{:S(2)}) async-start(), calls=%async_computation.17 | async-start | bytes 983040
  451.7 4.5 copy-start.31
  459.8 139.6 %reduce-scatter.19.cloned.1.call-start = ((), (), s32[]{:S(2)}) async-start(), calls=%async_computation.14 | async-start | bytes 2433024 | tf_op jit(solution)/shard_map/reduce_scatter | solution.py:351
  463.4 260.8 %reduce-scatter.33.cloned.1.call-start = ((), (), s32[]{:S(2)}) async-start(), calls=%async_computation.21 | async-start | bytes 7299072
  463.6 3.2 copy-start.8
  463.6 3.2 copy-start.13
  510.0 356.0 %reduce-scatter.21.cloned.1.call-start = ((), (), s32[]{:S(2)}) async-start(), calls=%async_computation.15 | async-start | bytes 9732096 | tf_op jit(solution)/shard_map/reduce_scatter | solution.py:351
  510.0 2.9 copy-start.6
  510.0 2.9 copy-start.30
  510.0 2.9 copy-start.56
  510.0 2.9 copy-start.60
  518.2 489.6 %reduce-scatter.23.cloned.1.call-start = ((), (), s32[]{:S(2)}) async-start(), calls=%async_computation.16 | async-start | bytes 9732096 | tf_op jit(solution)/shard_map/reduce_scatter | solution.py:351
  518.2 2.8 copy-start.23
  518.2 2.8 copy-start.28
  (39 other events, 65.4 us)
Sparse Core Ops, SparseCore 0:
  10.9 62.7 all-gather.6
  81.0 35.2 all-gather.8
  118.1 31.2 all-gather.16
  152.2 53.9 all-gather.10
  209.0 62.3 all-gather.12
  274.1 61.8 all-gather.14
  378.5 26.6 reduce-scatter.30
  408.0 27.2 reduce-scatter.28
  438.3 26.5 reduce-scatter.26
  467.6 26.1 reduce-scatter.24
  499.6 99.7 reduce-scatter.18
  605.5 118.6 reduce-scatter.32
  730.7 135.2 reduce-scatter.20
  872.3 135.4 reduce-scatter.22
